TPU v7x, 512 devices: a whole 4x4x16 slice. The times are simulated.
512 devices in a mesh: row: 32 (over x_lo, z), col: 16 (over x_hi, y, core).
Axes of the slice: x: 4 (x_hi: 2, x_lo: 2; x = x_hi * 2 + x_lo), y: 4, z: 16, core: 2. Of those that a mesh axis runs over, the one named last changes fastest.
Arguments:
- tokens: bfloat16 [256, 12288], P('row', 'col'), may hold values from -6 to 6
- past_tokens: bfloat16 [256, 12288], P('row', 'col'), may hold values from -6 to 6
- out_grad: bfloat16 [256, 12288], P('row', 'col'), may hold values from -3 to 3
- w_in: bfloat16 [12288, 24576], P('col', 'row'), may hold values from -0.0546875 to 0.0546875
- w_out: bfloat16 [24576, 12288], P('row', 'col'), may hold values from -0.0390625 to 0.0390625
Outputs:
- layer_out: bfloat16 [256, 12288], P('row', 'col')
- input_grad: bfloat16 [256, 12288], P('row', 'col')
- grad_w_in: bfloat16 [12288, 24576], P('col', 'row')
- grad_w_out: bfloat16 [24576, 12288], P('row', 'col')
All inputs are finite; a program needn't handle non-finite values.
Results may differ from a plain program's by a relative error of at most 0.005.
Values may be sent and summed in bfloat16 or wider, within the bound.
A program may use at most 64 MiB of HBM per device.

v0:
```python
import jax
import jax.numpy as jnp
from jax import lax
from jax.sharding import Mesh
from jax.sharding import PartitionSpec as P

ROW = ("row_0", "row_1")


def in_order(pieces, dim):
    pieces = jnp.moveaxis(pieces, 0, dim)
    shape = pieces.shape
    return pieces.reshape(*shape[:dim], shape[dim] * shape[dim + 1], *shape[dim + 2 :])


def stacked_from(shard, axes, order):
    pieces = shard[None]
    for k in order:
        pieces = lax.all_gather(pieces, axes[k], axis=0, tiled=True)
    carried = [lax.axis_size(axes[k]) for k in reversed(order)]
    pieces = pieces.reshape(*carried, *shard.shape)
    turned = sorted(range(len(order)), key=lambda place: order[len(order) - 1 - place])
    return pieces.transpose(*turned, *range(len(order), pieces.ndim)).reshape(-1, *shard.shape)


def gather_axes(shard, axes, order, dim):
    return in_order(stacked_from(shard, axes, order), dim)


def cut_along(shard, dim, length):
    shape = shard.shape
    pieces = shard.reshape(*shape[:dim], length, shape[dim] // length, *shape[dim + 1 :])
    return jnp.moveaxis(pieces, dim, 0)


def sent_and_summed(shard, axis, dim):
    pieces = cut_along(shard, dim, lax.axis_size(axis))
    arrived = lax.all_to_all(pieces, axis, split_axis=0, concat_axis=0, tiled=True)
    return arrived.sum(axis=0)


def sent_to_all(shard, axis):
    copies = jnp.broadcast_to(shard, (lax.axis_size(axis), *shard.shape))
    return lax.all_to_all(copies, axis, split_axis=0, concat_axis=0, tiled=True)


def gathered_copies(shard, axis, dim):
    return in_order(sent_to_all(shard, axis), dim)


def sent_together(arrays, axis, dim, along):
    both = jnp.concatenate(arrays, axis=along)
    out, at, gathered = (lax.all_gather(both, axis, axis=dim, tiled=True), 0, [])
    for a in arrays:
        gathered.append(lax.slice_in_dim(out, at, at + a.shape[along], axis=along))
        at += a.shape[along]
    return tuple(gathered)


def in_one_piece(arrays, axis, dim, along):
    widths = [a.shape[along] for a in arrays]
    both = jnp.concatenate(arrays, axis=along)
    out = lax.psum_scatter(both, axis, scatter_dimension=dim, tiled=True)
    return tuple(jnp.split(out, [sum(widths[:k]) for k in range(1, len(widths))], axis=along))


def gelu_parts(pre):
    cdf = 0.5 * (1.0 + jax.scipy.special.erf(pre * 0.7071067811865476))
    slope = cdf + pre * jnp.exp(-0.5 * pre * pre) * 0.3989422804014327
    return (pre * cdf, slope)


def local(tokens, past_tokens, out_grad, w_in, w_out):
    pre_part = jnp.dot(
        gather_axes(tokens, ROW, (0, 1), 0), w_in, preferred_element_type=jnp.float32
    )
    pre_share = sent_and_summed(pre_part, "col", 0)
    hidden_share = gelu_parts(pre_share)[0].astype(jnp.bfloat16)
    hidden_all = gathered_copies(hidden_share, "col", 0)
    block = hidden_all
    layer_out = sent_and_summed(
        jnp.dot(block, w_out, preferred_element_type=jnp.float32), ROW, 0
    ).astype(jnp.bfloat16)
    past_all, grad_all = sent_together((past_tokens, out_grad), ROW, 0, 1)
    past_part = jnp.dot(past_all, w_in, preferred_element_type=jnp.float32)
    back_part = lax.dot_general(
        grad_all, w_out, (((1,), (1,)), ((), ())), preferred_element_type=jnp.float32
    )
    past_share, back_share = in_one_piece((past_part, back_part), "col", 0, 1)
    act_share, slope = gelu_parts(past_share)
    act_local = act_share.astype(jnp.bfloat16)
    grad_local = (back_share * slope).astype(jnp.bfloat16)
    act_all, hidden_grad = sent_together((act_local, grad_local), "col", 0, 1)
    grad_w_out = lax.dot_general(
        act_all, grad_all, (((0,), (0,)), ((), ())), preferred_element_type=jnp.float32
    ).astype(jnp.bfloat16)
    grad_w_in = lax.dot_general(
        past_all, hidden_grad, (((0,), (0,)), ((), ())), preferred_element_type=jnp.float32
    ).astype(jnp.bfloat16)
    block = hidden_grad
    input_grad = sent_and_summed(
        lax.dot_general(block, w_in, (((1,), (1,)), ((), ())), preferred_element_type=jnp.float32),
        ROW,
        0,
    ).astype(jnp.bfloat16)
    return (layer_out, input_grad, grad_w_in, grad_w_out)


def solution(mesh):
    split = Mesh(mesh.devices.reshape(2, 16, mesh.shape["col"]), ("row_0", "row_1", "col"))
    return jax.shard_map(
        local,
        mesh=split,
        in_specs=(P(ROW, "col"), P(ROW, "col"), P(ROW, "col"), P("col", ROW), P(ROW, "col")),
        out_specs=(P(ROW, "col"), P(ROW, "col"), P("col", ROW), P(ROW, "col")),
        check_vma=False,
    )
```

profile of v0, /device:TPU:32, one launch (start us, length us, event | category | flops | bytes accessed | tf_op | source)
XLA Modules:
  0.0 314.2 jit_solution(4100335702246159757)
XLA Ops:
  7.2 0.0 copy-start
  7.2 4.7 %all-gather = bf16[16,768]{1,0:T(8,128)(2,1)S(1)} all-gather(bf16[8,768]{1,0:T(8,128)(2,1)} %param.5), channel_id=2, replica_groups=mesh['row_0'=2,'row_1'=16,'col'=16] {'row_0'}, dimensions={0}, use_global_device_ids=true | all-gather | bytes 36864 | tf_op jit(solution)/shard_map/all_gather | solution.py:19
  11.9 35.8 %all_gather.13 = bf16[32,8,768]{2,1,0:T(8,128)(2,1)S(1)} all-gather(bf16[2,8,768]{2,1,0:T(8,128)(2,1)S(1)} %bitcast.22), channel_id=1, replica_groups=mesh['row_0'=2,'row_1'=16,'col'=16] {'row_1'}, dimensions={0}, use_global_device_ids=true | all-gather | bytes 417792 | tf_op jit(solution)/shard_map/all_gather | solution.py:19
  47.8 0.0 copy-done
  47.8 1.4 fusion.2
  49.1 0.0 copy-start.3
  49.1 0.0 copy-start.4
  49.1 7.2 %all-to-all-start = ((f32[16,16,768]{2,1,0:T(8,128)}), f32[16,16,768]{2,1,0:T(8,128)}, u32[]{:S(2)}, u32[]{:S(2)}) async-start(f32[16,16,768]{2,1,0:T(8,128)} %fusion.2), calls=%async_computation | async-start | bytes 1572864 | tf_op jit(solution)/shard_map/all_to_all | solution.py:38
  56.4 0.0 copy-done.3
  56.4 0.0 copy-done.4
  56.4 64.7 %all_gather.14 = bf16[256,1536]{1,0:T(8,128)(2,1)S(1)} all-gather(bf16[8,1536]{1,0:T(8,128)(2,1)S(1)} %pad_maximum_fusion.2), channel_id=1, replica_groups=mesh['row_0'=2,'row_1'=16,'col'=16] {'row_0','row_1'}, dimensions={0}, use_global_device_ids=true | all-gather | bytes 811008 | tf_op jit(solution)/shard_map/all_gather | solution.py:53
  121.1 1.4 fusion.11
  122.4 0.0 copy-start.1
  122.4 0.0 all-to-all-done
  122.4 1.3 reduce_sum.27
  123.8 0.8 broadcast_in_dim.7
  124.5 7.2 %all-to-all-start.1 = ((bf16[16,16,768]{2,1,0:T(8,128)(2,1)}), bf16[16,16,768]{2,1,0:T(8,128)(2,1)S(1)}, u32[]{:S(2)}, u32[]{:S(2)}) async-start(bf16[16,16,768]{2,1,0:T(8,128)(2,1)} %broadcast_in_dim.7), calls=%async_computation.1 | async-start | bytes 786432 | tf_op jit(solution)/shard_map/all_to_all | solution.py:44
  131.8 0.0 reduce-scatter.2.cloned.1.call-start
  131.8 0.0 copy-done.1
  131.8 0.0 copy-start.2
  131.9 0.5 fusion.8
  132.4 0.6 copy-done.2
  133.0 1.3 pad_maximum_fusion
  134.3 0.0 reduce-scatter.2.cloned.1.call-update
  134.3 8.4 %all-to-all-done.1 = bf16[16,16,768]{2,1,0:T(8,128)(2,1)S(1)} async-done(((bf16[16,16,768]{2,1,0:T(8,128)(2,1)}), bf16[16,16,768]{2,1,0:T(8,128)(2,1)S(1)}, u32[]{:S(2)}, u32[]{:S(2)}) %all-to-all-start.1) | async-done | bytes 393248 | tf_op jit(solution)/shard_map/all_to_all | solution.py:44
  142.7 1.4 fusion
  144.1 4.4 %all-to-all-start.2 = ((f32[32,8,768]{2,1,0:T(8,128)}), f32[32,8,768]{2,1,0:T(8,128)S(1)}, u32[]{:S(2)}, u32[]{:S(2)}) async-start(f32[32,8,768]{2,1,0:T(8,128)} %fusion), calls=%async_computation.2 | async-start | bytes 1572864 | tf_op jit(solution)/shard_map/all_to_all | solution.py:38
  148.5 73.4 %reduce-scatter.2.cloned.1.call-done = f32[16,1536]{1,0:T(8,128)} async-done(((f32[256,1536]{1,0:T(8,128)}), f32[16,1536]{1,0:T(8,128)}) %reduce-scatter.2.cloned.1.call-update) | async-done | bytes 98320 | tf_op jit(solution)/shard_map/reduce_scatter | solution.py:63
  221.8 0.9 multiply_convert_fusion
  222.7 23.7 %all_gather.15 = bf16[256,1536]{1,0:T(8,128)(2,1)S(1)} all-gather(bf16[16,1536]{1,0:T(8,128)(2,1)S(1)} %pad_maximum_fusion.1), channel_id=1, replica_groups=mesh['row_0'=2,'row_1'=16,'col'=16] {'col'}, dimensions={0}, use_global_device_ids=true | all-gather | bytes 835584 | tf_op jit(solution)/shard_map/all_gather | solution.py:53
  246.4 1.4 convolution_bitcast_fusion
  247.8 0.0 all-to-all-done.2
  247.8 13.6 %all-to-all-start.3 = ((f32[32,8,768]{2,1,0:T(8,128)}), f32[32,8,768]{2,1,0:T(8,128)}, u32[]{:S(2)}, u32[]{:S(2)}) async-start(f32[32,8,768]{2,1,0:T(8,128)} %convolution_bitcast_fusion), calls=%async_computation.4 | async-start | bytes 1572864 | tf_op jit(solution)/shard_map/all_to_all | solution.py:38
  261.4 1.5 convolution_convert_fusion
  263.0 1.5 convolution_convert_fusion.1
  264.5 0.7 reduce_sum.28
  265.1 40.4 %all-to-all-done.3 = f32[32,8,768]{2,1,0:T(8,128)} async-done(((f32[32,8,768]{2,1,0:T(8,128)}), f32[32,8,768]{2,1,0:T(8,128)}, u32[]{:S(2)}, u32[]{:S(2)}) %all-to-all-start.3) | async-done | bytes 786464 | tf_op jit(solution)/shard_map/all_to_all | solution.py:38
  305.6 1.8 reduce_sum.29
  (4 shorter events, 0.1 us)
Async XLA Ops:
  7.2 40.6 %copy-start = (bf16[768,768]{1,0:T(8,128)(2,1)S(1)}, bf16[768,768]{1,0:T(8,128)(2,1)}, u32[]{:S(2)}) copy-start(bf16[768,768]{1,0:T(8,128)(2,1)} %param.8) | copy-start | bytes 3538948
  49.1 7.2 %copy-start.3 = (bf16[8,768]{1,0:T(8,128)(2,1)S(1)}, bf16[8,768]{1,0:T(8,128)(2,1)}, u32[]{:S(2)}) copy-start(bf16[8,768]{1,0:T(8,128)(2,1)} %param.7) | copy-start | bytes 36868
  49.1 7.2 %copy-start.4 = (bf16[8,768]{1,0:T(8,128)(2,1)S(1)}, bf16[8,768]{1,0:T(8,128)(2,1)}, u32[]{:S(2)}) copy-start(bf16[8,768]{1,0:T(8,128)(2,1)} %param.6) | copy-start | bytes 36868
  49.1 73.3 %all-to-all-start = ((f32[16,16,768]{2,1,0:T(8,128)}), f32[16,16,768]{2,1,0:T(8,128)}, u32[]{:S(2)}, u32[]{:S(2)}) async-start(f32[16,16,768]{2,1,0:T(8,128)} %fusion.2), calls=%async_computation | async-start | bytes 1572864 | tf_op jit(solution)/shard_map/all_to_all | solution.py:38
  122.4 9.4 %copy-start.1 = (bf16[768,768]{1,0:T(8,128)(2,1)S(1)}, bf16[768,768]{1,0:T(8,128)(2,1)}, u32[]{:S(2)}) copy-start(bf16[768,768]{1,0:T(8,128)(2,1)} %param.9) | copy-start | bytes 3538948
  124.5 18.2 %all-to-all-start.1 = ((bf16[16,16,768]{2,1,0:T(8,128)(2,1)}), bf16[16,16,768]{2,1,0:T(8,128)(2,1)S(1)}, u32[]{:S(2)}, u32[]{:S(2)}) async-start(bf16[16,16,768]{2,1,0:T(8,128)(2,1)} %broadcast_in_dim.7), calls=%async_computation.1 | async-start | bytes 786432 | tf_op jit(solution)/shard_map/all_to_all | solution.py:44
  131.8 90.1 %reduce-scatter.2.cloned.1.call-start = ((), (), s32[]{:S(2)}) async-start(), calls=%async_computation.5 | async-start | bytes 1671168 | tf_op jit(solution)/shard_map/reduce_scatter | solution.py:63
  131.8 1.1 copy-start.2
  144.1 103.7 %all-to-all-start.2 = ((f32[32,8,768]{2,1,0:T(8,128)}), f32[32,8,768]{2,1,0:T(8,128)S(1)}, u32[]{:S(2)}, u32[]{:S(2)}) async-start(f32[32,8,768]{2,1,0:T(8,128)} %fusion), calls=%async_computation.2 | async-start | bytes 1572864 | tf_op jit(solution)/shard_map/all_to_all | solution.py:38
  247.8 57.8 %all-to-all-start.3 = ((f32[32,8,768]{2,1,0:T(8,128)}), f32[32,8,768]{2,1,0:T(8,128)}, u32[]{:S(2)}, u32[]{:S(2)}) async-start(f32[32,8,768]{2,1,0:T(8,128)} %convolution_bitcast_fusion), calls=%async_computation.4 | async-start | bytes 1572864 | tf_op jit(solution)/shard_map/all_to_all | solution.py:38
Sparse Core Ops, SparseCore 0:
  137.4 84.4 reduce-scatter.1
where the time goes:
time: 315 us; the launch traced here: 314 us
  blocking collectives  129 us (41%)
  waiting for transfers between devices  122 us (39%)
  starting transfers between devices  32.5 us (10%)
  between operations  14.2 us (5%)
  matrix products  9.03 us (3%)
  other arithmetic  5.96 us (2%)
    all_gather x2, blocking collectives, sent_together(): lax.all_gather(both, axis, axis=dim, tiled=True)  88.3 us
    reduce_scatter x1, waiting for transfers between devices, in_one_piece(): out = lax.psum_scatter(both, axis, scatter_dimension=dim, tiled=True)  73.4 us
    all_gather x2, blocking collectives, stacked_from(): pieces = lax.all_gather(pieces, axes[k], axis=0, tiled=True)  40.6 us
    all_to_all x3, waiting for transfers between devices, sent_and_summed(): lax.all_to_all(pieces, axis, split_axis=0, concat_axis=0, tiled=True)  40.4 us
    all_to_all x3, starting transfers between devices, sent_and_summed(): lax.all_to_all(pieces, axis, split_axis=0, concat_axis=0, tiled=True)  25.3 us
    all_to_all x1, waiting for transfers between devices, sent_to_all(): return lax.all_to_all(copies, axis, split_axis=0, concat_axis=0, tiled=True)  8.37 us
    all_to_all x1, starting transfers between devices, sent_to_all(): return lax.all_to_all(copies, axis, split_axis=0, concat_axis=0, tiled=True)  7.25 us
  transfers between devices with their start and end apart: 5, of which 3 were waited for; matrix products, arithmetic and copies ran while one was open for 3% of the time, Pallas kernels for 0%

commit v1 on v0

--- a/solution.py
+++ b/solution.py
@@ -16,7 +16,9 @@
 def stacked_from(shard, axes, order):
     pieces = shard[None]
     for k in order:
-        pieces = lax.all_gather(pieces, axes[k], axis=0, tiled=True)
+        pieces = jnp.concatenate(
+            lax.all_to_all(jnp.stack([pieces] * lax.axis_size(axes[k])), axes[k], 0, 0), axis=0
+        )
     carried = [lax.axis_size(axes[k]) for k in reversed(order)]
     pieces = pieces.reshape(*carried, *shard.shape)
     turned = sorted(range(len(order)), key=lambda place: order[len(order) - 1 - place])

time: 315 us -> 336 us (1.067)
  waiting for transfers between devices: 122 us -> 150 us
  blocking collectives: 129 us -> 117 us
    all_gather x2 -> x0, blocking collectives: 40.6 us -> none  [stacked_from(): pieces = lax.all_gather(pieces, axes[k], axis=0, tiled=True)]
    all_to_all x3 -> x2, waiting for transfers between devices: 40.4 us -> 80.8 us  [sent_and_summed(): lax.all_to_all(pieces, axis, split_axis=0, concat_axis=0, tiled=True)]
    all_to_all x0 -> x1, blocking collectives: none -> 22 us  [sent_and_summed(): lax.all_to_all(pieces, axis, split_axis=0, concat_axis=0, tiled=True)]
    reduce_scatter x1, waiting for transfers between devices: 73.4 us -> 54.7 us  [in_one_piece(): out = lax.psum_scatter(both, axis, scatter_dimension=dim, tiled=True)]
    all_to_all x0 -> x2, waiting for transfers between devices: none -> 14.4 us  [stacked_from(): lax.all_to_all(jnp.stack([pieces] * lax.axis_size(axes[k])), axes[k], 0, 0)]
    all_to_all x0 -> x2, starting transfers between devices: none -> 12.7 us  [stacked_from(): lax.all_to_all(jnp.stack([pieces] * lax.axis_size(axes[k])), axes[k], 0, 0)]
    all_to_all x1, waiting for transfers between devices: 8.37 us -> 0.01 us  [sent_to_all(): return lax.all_to_all(copies, axis, split_axis=0, concat_axis=0, tiled=True)]
    all_to_all x3 -> x2, starting transfers between devices: 25.3 us -> 18 us  [sent_and_summed(): lax.all_to_all(pieces, axis, split_axis=0, concat_axis=0, tiled=True)]
  transfers between devices with their start and end apart: 5 -> 6, of which waited for: 3 -> 4; matrix products, arithmetic and copies ran while one was open for 3% -> 4% of each run, Pallas kernels for 0% -> 0%
where the time goes in v1:
time: 336 us; the launch traced here: 335 us
  waiting for transfers between devices  150 us (45%)
  blocking collectives  117 us (35%)
  starting transfers between devices  34.3 us (10%)
  between operations  14.1 us (4%)
  matrix products  9.55 us (3%)
  other arithmetic  6.87 us (2%)
    all_gather x2, blocking collectives, sent_together(): lax.all_gather(both, axis, axis=dim, tiled=True)  95.4 us
    all_to_all x2, waiting for transfers between devices, sent_and_summed(): lax.all_to_all(pieces, axis, split_axis=0, concat_axis=0, tiled=True)  80.8 us
    reduce_scatter x1, waiting for transfers between devices, in_one_piece(): out = lax.psum_scatter(both, axis, scatter_dimension=dim, tiled=True)  54.7 us
    all_to_all x1, blocking collectives, sent_and_summed(): lax.all_to_all(pieces, axis, split_axis=0, concat_axis=0, tiled=True)  22 us
    all_to_all x2, starting transfers between devices, sent_and_summed(): lax.all_to_all(pieces, axis, split_axis=0, concat_axis=0, tiled=True)  18 us
    all_to_all x2, waiting for transfers between devices, stacked_from(): lax.all_to_all(jnp.stack([pieces] * lax.axis_size(axes[k])), axes[k], 0, 0)  14.4 us
    all_to_all x2, starting transfers between devices, stacked_from(): lax.all_to_all(jnp.stack([pieces] * lax.axis_size(axes[k])), axes[k], 0, 0)  12.7 us
  transfers between devices with their start and end apart: 6, of which 4 were waited for; matrix products, arithmetic and copies ran while one was open for 4% of the time, Pallas kernels for 0%

profile of v1, /device:TPU:32, one launch (start us, length us, event | category | flops | bytes accessed | tf_op | source)
XLA Modules:
  0.0 335.2 jit_solution(10996247170398883568)
XLA Ops:
  7.2 0.0 copy-start
  7.2 1.4 pad_maximum_fusion.2
  8.6 3.2 all-to-all-start
  11.9 0.7 pad_maximum_fusion.3
  12.6 71.7 %all_gather.6 = bf16[256,1536]{1,0:T(8,128)(2,1)S(1)} all-gather(bf16[8,1536]{1,0:T(8,128)(2,1)S(1)} %pad_maximum_fusion.3), channel_id=1, replica_groups=mesh['row_0'=2,'row_1'=16,'col'=16] {'row_0','row_1'}, dimensions={0}, use_global_device_ids=true | all-gather | bytes 811008 | tf_op jit(solution)/shard_map/all_gather | solution.py:55
  84.3 0.0 copy-done
  84.3 1.4 fusion.11
  85.6 0.0 copy-start.1
  85.6 0.0 all-to-all-done
  85.7 0.8 stack.7
  86.4 9.5 %all-to-all-start.1 = ((bf16[16,2,8,768]{3,2,1,0:T(8,128)(2,1)}), bf16[16,2,8,768]{3,2,1,0:T(8,128)(2,1)S(1)}, u32[]{:S(2)}, u32[]{:S(2)}) async-start(bf16[16,2,8,768]{3,2,1,0:T(8,128)(2,1)} %stack.7), calls=%async_computation.1 | async-start | bytes 786432 | tf_op jit(solution)/shard_map/all_to_all | solution.py:20
  95.9 0.0 reduce-scatter.2.cloned.1.call-start
  95.9 0.0 copy-done.1
  95.9 0.0 copy-start.2
  96.0 0.5 fusion.8
  96.5 0.6 copy-done.2
  97.1 1.3 pad_maximum_fusion
  98.4 0.0 reduce-scatter.2.cloned.1.call-update
  98.4 14.4 %all-to-all-done.1 = bf16[16,2,8,768]{3,2,1,0:T(8,128)(2,1)S(1)} async-done(((bf16[16,2,8,768]{3,2,1,0:T(8,128)(2,1)}), bf16[16,2,8,768]{3,2,1,0:T(8,128)(2,1)S(1)}, u32[]{:S(2)}, u32[]{:S(2)}) %all-to-all-start.1) | async-done | bytes 393248 | tf_op jit(solution)/shard_map/all_to_all | solution.py:20
  112.9 0.5 fusion.2
  113.4 22.0 %all_to_all.30 = f32[16,16,768]{2,1,0:T(8,128)S(1)} all-to-all(f32[16,16,768]{2,1,0:T(8,128)S(1)} %fusion.2), channel_id=1, replica_groups=mesh['row_0'=2,'row_1'=16,'col'=16] {'col'}, dimensions={0} | all-to-all | bytes 1572864 | tf_op jit(solution)/shard_map/all_to_all | solution.py:40
  135.4 0.8 broadcast_in_dim.3
  136.2 3.6 %all-to-all-start.3 = ((bf16[16,16,768]{2,1,0:T(8,128)(2,1)}), bf16[16,16,768]{2,1,0:T(8,128)(2,1)S(1)}, u32[]{:S(2)}, u32[]{:S(2)}) async-start(bf16[16,16,768]{2,1,0:T(8,128)(2,1)} %broadcast_in_dim.3), calls=%async_computation.3 | async-start | bytes 786432 | tf_op jit(solution)/shard_map/all_to_all | solution.py:46
  139.8 54.7 %reduce-scatter.2.cloned.1.call-done = f32[16,1536]{1,0:T(8,128)} async-done(((f32[256,1536]{1,0:T(8,128)}), f32[16,1536]{1,0:T(8,128)}) %reduce-scatter.2.cloned.1.call-update) | async-done | bytes 98320 | tf_op jit(solution)/shard_map/reduce_scatter | solution.py:65
  194.5 0.9 multiply_convert_fusion
  195.4 23.7 %all_gather.7 = bf16[256,1536]{1,0:T(8,128)(2,1)S(1)} all-gather(bf16[16,1536]{1,0:T(8,128)(2,1)S(1)} %pad_maximum_fusion.1), channel_id=1, replica_groups=mesh['row_0'=2,'row_1'=16,'col'=16] {'col'}, dimensions={0}, use_global_device_ids=true | all-gather | bytes 835584 | tf_op jit(solution)/shard_map/all_gather | solution.py:55
  219.1 1.4 convolution_bitcast_fusion
  220.5 0.0 all-to-all-done.3
  220.5 0.0 copy-start.3
  220.5 0.7 copy-done.3
  221.2 13.6 %all-to-all-start.5 = ((f32[32,8,768]{2,1,0:T(8,128)}), f32[32,8,768]{2,1,0:T(8,128)S(1)}, u32[]{:S(2)}, u32[]{:S(2)}) async-start(f32[32,8,768]{2,1,0:T(8,128)} %convolution_bitcast_fusion), calls=%async_computation.6 | async-start | bytes 1572864 | tf_op jit(solution)/shard_map/all_to_all | solution.py:40
  234.8 2.8 fusion
  237.6 41.3 %all-to-all-done.5 = f32[32,8,768]{2,1,0:T(8,128)S(1)} async-done(((f32[32,8,768]{2,1,0:T(8,128)}), f32[32,8,768]{2,1,0:T(8,128)S(1)}, u32[]{:S(2)}, u32[]{:S(2)}) %all-to-all-start.5) | async-done | bytes 786464 | tf_op jit(solution)/shard_map/all_to_all | solution.py:40
  278.9 4.4 %all-to-all-start.4 = ((f32[32,8,768]{2,1,0:T(8,128)}), f32[32,8,768]{2,1,0:T(8,128)}, u32[]{:S(2)}, u32[]{:S(2)}) async-start(f32[32,8,768]{2,1,0:T(8,128)} %fusion), calls=%async_computation.4 | async-start | bytes 1572864 | tf_op jit(solution)/shard_map/all_to_all | solution.py:40
  283.3 1.5 convolution_convert_fusion
  284.8 1.5 convolution_convert_fusion.1
  286.4 0.7 reduce_sum.29
  287.0 39.5 %all-to-all-done.4 = f32[32,8,768]{2,1,0:T(8,128)} async-done(((f32[32,8,768]{2,1,0:T(8,128)}), f32[32,8,768]{2,1,0:T(8,128)}, u32[]{:S(2)}, u32[]{:S(2)}) %all-to-all-start.4) | async-done | bytes 786464 | tf_op jit(solution)/shard_map/all_to_all | solution.py:40
  326.5 1.8 reduce_sum.28
  (4 shorter events, 0.1 us)
Async XLA Ops:
  7.2 77.1 %copy-start = (bf16[768,768]{1,0:T(8,128)(2,1)S(1)}, bf16[768,768]{1,0:T(8,128)(2,1)}, u32[]{:S(2)}) copy-start(bf16[768,768]{1,0:T(8,128)(2,1)} %param.8) | copy-start | bytes 3538948
  8.6 77.0 %all-to-all-start = ((bf16[2,1,8,768]{3,2,1,0:T(8,128)(2,1)}), bf16[2,1,8,768]{3,2,1,0:T(8,128)(2,1)S(1)}, u32[]{:S(2)}, u32[]{:S(2)}) async-start(bf16[2,1,8,768]{3,2,1,0:T(8,128)(2,1)} %pad_maximum_fusion.2), calls=%async_computation | async-start | bytes 49152 | tf_op jit(solution)/shard_map/all_to_all | solution.py:20
  85.6 10.3 %copy-start.1 = (bf16[768,768]{1,0:T(8,128)(2,1)S(1)}, bf16[768,768]{1,0:T(8,128)(2,1)}, u32[]{:S(2)}) copy-start(bf16[768,768]{1,0:T(8,128)(2,1)} %param.9) | copy-start | bytes 3538948
  86.4 26.5 %all-to-all-start.1 = ((bf16[16,2,8,768]{3,2,1,0:T(8,128)(2,1)}), bf16[16,2,8,768]{3,2,1,0:T(8,128)(2,1)S(1)}, u32[]{:S(2)}, u32[]{:S(2)}) async-start(bf16[16,2,8,768]{3,2,1,0:T(8,128)(2,1)} %stack.7), calls=%async_computation.1 | async-start | bytes 786432 | tf_op jit(solution)/shard_map/all_to_all | solution.py:20
  95.9 98.6 %reduce-scatter.2.cloned.1.call-start = ((), (), s32[]{:S(2)}) async-start(), calls=%async_computation.7 | async-start | bytes 1671168 | tf_op jit(solution)/shard_map/reduce_scatter | solution.py:65
  95.9 1.1 copy-start.2
  136.2 84.2 %all-to-all-start.3 = ((bf16[16,16,768]{2,1,0:T(8,128)(2,1)}), bf16[16,16,768]{2,1,0:T(8,128)(2,1)S(1)}, u32[]{:S(2)}, u32[]{:S(2)}) async-start(bf16[16,16,768]{2,1,0:T(8,128)(2,1)} %broadcast_in_dim.3), calls=%async_computation.3 | async-start | bytes 786432 | tf_op jit(solution)/shard_map/all_to_all | solution.py:46
  220.5 0.7 copy-start.3
  221.2 57.7 %all-to-all-start.5 = ((f32[32,8,768]{2,1,0:T(8,128)}), f32[32,8,768]{2,1,0:T(8,128)S(1)}, u32[]{:S(2)}, u32[]{:S(2)}) async-start(f32[32,8,768]{2,1,0:T(8,128)} %convolution_bitcast_fusion), calls=%async_computation.6 | async-start | bytes 1572864 | tf_op jit(solution)/shard_map/all_to_all | solution.py:40
  278.9 47.7 %all-to-all-start.4 = ((f32[32,8,768]{2,1,0:T(8,128)}), f32[32,8,768]{2,1,0:T(8,128)}, u32[]{:S(2)}, u32[]{:S(2)}) async-start(f32[32,8,768]{2,1,0:T(8,128)} %fusion), calls=%async_computation.4 | async-start | bytes 1572864 | tf_op jit(solution)/shard_map/all_to_all | solution.py:40
Sparse Core Ops, SparseCore 0:
  101.5 92.9 reduce-scatter.1
